TPU v7x, 512 devices: a whole 4x8x8 slice. The times are simulated.
512 devices in a mesh: expert: 8 (over x, z_hi), tensor: 64 (over y, z_lo, core).
Axes of the slice: x: 4, y: 8, z: 8 (z_hi: 2, z_lo: 4; z = z_hi * 4 + z_lo), core: 2. Of those that a mesh axis runs over, the one named last changes fastest.
Arguments:
- tokens: bfloat16 [384, 6144], P('expert', 'tensor'), may hold values from -6 to 6
- expert_ids: int32 [384, 2], P('expert'), may hold values from 0 to 7, as said below
- route_weight: int32 [384, 2], P('expert'), may hold values from 1 to 4095
- gate_weight: bfloat16 [8, 6144, 8192], P('expert', None, 'tensor'), may hold values from -0.078125 to 0.078125
- up_weight: bfloat16 [8, 6144, 8192], P('expert', None, 'tensor'), may hold values from -0.078125 to 0.078125
- down_weight: bfloat16 [8, 8192, 6144], P('expert', 'tensor'), may hold values from -0.0625 to 0.0625
Outputs:
- mixed: bfloat16 [384, 6144], P('expert', 'tensor')
- expert_load: float32 [2, 8], replicated
Inputs may be any that keep to these rules, and one draw needn't show every extreme that they name: `expert_ids`: each row names two different experts. The hot expert is the one named in the first column of the first row of every aligned block of 48 rows (the tokens of one expert group), the same in all blocks. In each block exactly 42 rows name the hot expert, in either column; every other expert is named by 7 or 8 rows of each block, and by exactly 8 rows in some.
All inputs are finite; a program needn't handle non-finite values.
Results may differ from a plain program's by a relative error of at most 0.005.
Values may be sent and summed in bfloat16 or wider, within the bound.
A program may use at most 64 MiB of HBM per device.

v0:
```python
import jax
import jax.numpy as jnp
from jax import lax
from jax.sharding import PartitionSpec as P


def filled_up(lines, length):
    spare = -len(lines) % length
    return jnp.pad(lines, [(0, spare)] + [(0, 0)] * (lines.ndim - 1))


def from_root(value, axis, root):
    lines = jnp.where(lax.axis_index(axis) == root, value, jnp.zeros_like(value)).reshape(
        -1, *value.shape[1:][-1:]
    )
    padded = filled_up(lines, lax.axis_size(axis))
    own = lax.psum_scatter(padded, axis, scatter_dimension=0, tiled=True)
    return lax.all_gather(own, axis, axis=0, tiled=True)[: len(lines)].reshape(value.shape)


def gather_turned(arrays, axis, dims):
    turned = [jnp.moveaxis(a, dim, 0) for a, dim in zip(arrays, dims)]
    widths = [t[0].size for t in turned]
    both = jnp.concatenate([t.reshape(-1, w) for t, w in zip(turned, widths)], axis=1)
    out = lax.all_gather(both, axis, axis=0, tiled=True)
    blocks = jnp.split(out, [sum(widths[:k]) for k in range(1, len(widths))], axis=1)
    return tuple(
        (
            jnp.moveaxis(b.reshape(-1, *t.shape[1:]), 0, dim)
            for b, t, dim in zip(blocks, turned, dims)
        )
    )


def split_up(value, dim, length):
    lengths = value.shape
    blocks = value.reshape(*lengths[:dim], length, lengths[dim] // length, *lengths[dim + 1 :])
    return jnp.moveaxis(blocks, dim, 0)


def sum_at_owner(value, axis, dim):
    length = lax.axis_size(axis)
    blocks = lax.all_to_all(split_up(value, dim, length), axis, 0, 0, tiled=True)
    return jnp.sum(blocks, axis=0)


def from_everyone(value, axis):
    copies = jnp.broadcast_to(value, (lax.axis_size(axis), *value.shape))
    return lax.all_to_all(copies, axis, split_axis=0, concat_axis=0, tiled=True)


def of_everyone(value, axis):
    return from_everyone(value, axis).sum(axis=0)


def swiglu(gate_value, up_value):
    return (jax.nn.silu(gate_value) * up_value).astype(jnp.bfloat16)


def matmul(left, right):
    return jnp.dot(left, right, preferred_element_type=jnp.float32)


def route_stats(id_block, raw_block, labels):
    weights = raw_block.astype(jnp.float32)
    route_share = weights / jnp.sum(weights, axis=1, keepdims=True)
    flat_chosen = (
        (id_block[:, :, None] == labels[None, None, :])
        .astype(jnp.int32)
        .reshape(-1, labels.shape[0])
    )
    chosen_float = flat_chosen.astype(jnp.float32)
    stats = jnp.stack(
        [jnp.sum(chosen_float, axis=0), jnp.sum(route_share.reshape(-1, 1) * chosen_float, axis=0)]
    )
    return (route_share, flat_chosen, stats)


def local(tokens, expert_ids, route_weight, gate_weight, up_weight, down_weight):
    tok_rows = expert_ids.shape[0]
    experts = lax.axis_size("expert") * gate_weight.shape[0]
    hot_rows = tok_rows - tok_rows // 8 * min(experts - 2, 1)
    capacity = (2 * tok_rows - hot_rows + experts - 2) // (experts - 1)
    hot_id = expert_ids[0, 0]
    own_gate = gate_weight[0]
    own_up = up_weight[0]
    own_down = down_weight[0]
    hot_gate_w, hot_up_w, hot_down_w = (
        from_root(own_gate, "expert", hot_id),
        from_root(own_up, "expert", hot_id),
        from_root(own_down, "expert", hot_id),
    )
    labels = jnp.arange(experts, dtype=jnp.int32)
    route_share, flat_chosen, local_stats = route_stats(expert_ids, route_weight, labels)
    cold_chosen = flat_chosen * (labels != hot_id).astype(jnp.int32)[None, :]
    slot_index = jnp.sum((jnp.cumsum(cold_chosen, axis=0) - 1) * cold_chosen, axis=1)
    is_live = jnp.sum(cold_chosen, axis=1)
    target = jnp.sum(cold_chosen * labels[None, :], axis=1) * capacity + slot_index
    buffer_rows = jnp.arange(experts * capacity, dtype=jnp.int32)
    cold_pick = ((target[None, :] == buffer_rows[:, None]) & (is_live[None, :] == 1)).astype(
        jnp.bfloat16
    )
    cold_pick = jnp.sum(cold_pick.reshape(experts * capacity, tok_rows, 2), axis=2)
    hot_match = (expert_ids == hot_id).astype(jnp.int32)
    hot_flag = jnp.sum(hot_match, axis=1)
    hot_rank = jnp.cumsum(hot_flag) - 1
    hot_slots = jnp.arange(hot_rows, dtype=jnp.int32)
    hot_pick = ((hot_rank[None, :] == hot_slots[:, None]) & (hot_flag[None, :] == 1)).astype(
        jnp.bfloat16
    )
    feature_width = tokens.shape[1]
    cold_send = (
        matmul(cold_pick, tokens).astype(jnp.bfloat16).reshape(experts, capacity, feature_width)
    )
    cold_recv = lax.all_to_all(
        cold_send, "expert", split_axis=0, concat_axis=0, tiled=True
    ).reshape(experts * capacity, feature_width)
    hot_input = matmul(hot_pick, tokens).astype(jnp.bfloat16)
    cold_piece, hot_piece = gather_turned((cold_recv, hot_input), "tensor", (1, 1))
    cold_gate = matmul(cold_piece, own_gate)
    cold_up = matmul(cold_piece, own_up)
    hot_gate = matmul(hot_piece, hot_gate_w)
    hot_up = matmul(hot_piece, hot_up_w)
    cold_part = matmul(swiglu(cold_gate, cold_up), own_down)
    hot_part = matmul(swiglu(hot_gate, hot_up), hot_down_w)
    model_width = cold_part.shape[1]
    returned = lax.all_to_all(
        cold_part.reshape(experts, capacity, model_width),
        "expert",
        split_axis=0,
        concat_axis=0,
        tiled=True,
    ).reshape(experts * capacity, model_width)
    assign_weight = route_share.reshape(2 * tok_rows) * is_live.astype(jnp.float32)
    cold_out = jnp.sum(
        (returned[target] * assign_weight[:, None]).reshape(tok_rows, 2, model_width), axis=1
    )
    hot_weight = jnp.sum(route_share * hot_match.astype(jnp.float32), axis=1)
    hot_out = hot_part[jnp.clip(hot_rank, 0, hot_rows - 1)] * hot_weight[:, None]
    mixed = sum_at_owner(cold_out + hot_out, "tensor", 1).astype(jnp.bfloat16)
    expert_load = of_everyone(local_stats, "expert") / tok_rows
    return (mixed, expert_load)


def solution(mesh):
    placed = (
        P("expert", "tensor"),
        P("expert", None),
        P("expert", None),
        P("expert", None, "tensor"),
        P("expert", None, "tensor"),
        P("expert", "tensor", None),
    )
    return jax.shard_map(
        local, mesh=mesh, in_specs=placed, out_specs=(P("expert", "tensor"), P()), check_vma=False
    )
```

profile of v0, /device:TPU:1, one launch (start us, length us, event | category | flops | bytes accessed | tf_op | source)
XLA Modules:
  0.0 469.7 jit_solution(4374038837522308300)
XLA Ops:
  9.9 2.7 bitcast_select_fusion.2
  12.6 1.3 copy-done.4
  14.0 1.3 bitcast_select_fusion
  18.6 13.3 %all-to-all-start = ((bf16[8,8,96]{2,1,0:T(8,128)(2,1)}), bf16[8,8,96]{2,1,0:T(8,128)(2,1)S(1)}, u32[]{:S(2)}, u32[]{:S(2)}) async-start(bf16[8,8,96]{2,1,0:T(8,128)(2,1)} %fusion.28), calls=%async_computation | async-start | bytes 32768 | tf_op jit(solution)/shard_map/all_to_all | solution.py:115
  33.0 7.8 %all-to-all-done = bf16[8,8,96]{2,1,0:T(8,128)(2,1)S(1)} async-done(((bf16[8,8,96]{2,1,0:T(8,128)(2,1)}), bf16[8,8,96]{2,1,0:T(8,128)(2,1)S(1)}, u32[]{:S(2)}, u32[]{:S(2)}) %all-to-all-start) | async-done | bytes 12320 | tf_op jit(solution)/shard_map/all_to_all | solution.py:115
  43.0 72.0 %reduce-scatter.4.cloned.1.call-done = bf16[768,128]{1,0:T(8,128)(2,1)} async-done(((bf16[6144,128]{1,0:T(8,128)(2,1)}), bf16[768,128]{1,0:T(8,128)(2,1)}) %reduce-scatter.4.cloned.1.call-update) | async-done | bytes 196624 | tf_op jit(solution)/shard_map/reduce_scatter | solution.py:17
  115.1 98.7 %reduce-scatter.8.cloned.1.call-done = bf16[16,6144]{1,0:T(8,128)(2,1)} async-done(((bf16[128,6144]{1,0:T(8,128)(2,1)}), bf16[16,6144]{1,0:T(8,128)(2,1)}) %reduce-scatter.8.cloned.1.call-update) | async-done | bytes 196624 | tf_op jit(solution)/shard_map/reduce_scatter | solution.py:17
  213.8 2.1 fusion.4
  215.9 4.0 fusion
  219.9 3.7 all-to-all-start.1
  223.7 107.7 %reduce-scatter.6.cloned.1.call-done = bf16[768,128]{1,0:T(8,128)(2,1)} async-done(((bf16[6144,128]{1,0:T(8,128)(2,1)}), bf16[768,128]{1,0:T(8,128)(2,1)}) %reduce-scatter.6.cloned.1.call-update) | async-done | bytes 196624 | tf_op jit(solution)/shard_map/reduce_scatter | solution.py:17
  333.4 3.6 all-to-all-start.3
  337.0 2.7 gather_fusion
  339.7 3.8 gather.11
  343.5 5.1 %multiply_reduce_fusion = f32[48,6144]{1,0:T(8,128)S(1)} fusion(f32[48,2,6144]{2,1,0:T(2,128)} %gather.11, f32[48,2]{1,0:T(8,128)S(1)} %copy.64), kind=kLoop, calls=%fused_computation.2 | loop fusion | flops 884736 | bytes 3539328 | tf_op jit(solution)/shard_map/reduce_sum | solution.py:135
  348.6 1.8 reduce_sum.120
  350.4 2.4 fusion.8
  352.9 49.2 %all-gather.9.cloned.1.call-done = bf16[6144,128]{1,0:T(8,128)(2,1)} async-done(((bf16[768,128]{1,0:T(8,128)(2,1)}), bf16[6144,128]{1,0:T(8,128)(2,1)}) %all-gather.9.cloned.1.call-update) | async-done | bytes 1572880 | tf_op jit(solution)/shard_map/all_gather | solution.py:18
  402.1 3.2 fusion.36
  405.3 1.9 gather_fusion.1
  407.3 2.0 gather.13
  409.5 2.1 copy.65
  411.6 10.4 %all-to-all-start.2 = ((f32[64,48,96]{2,1,0:T(8,128)}), f32[64,48,96]{2,1,0:T(8,128)S(1)}, u32[]{:S(2)}, u32[]{:S(2)}) async-start(f32[64,48,96]{2,1,0:T(8,128)} %copy.65), calls=%async_computation.5 | async-start | bytes 3145728 | tf_op jit(solution)/shard_map/all_to_all | solution.py:43
  422.5 39.1 %all-to-all-done.2 = f32[64,48,96]{2,1,0:T(8,128)S(1)} async-done(((f32[64,48,96]{2,1,0:T(8,128)}), f32[64,48,96]{2,1,0:T(8,128)S(1)}, u32[]{:S(2)}, u32[]{:S(2)}) %all-to-all-start.2) | async-done | bytes 1179680 | tf_op jit(solution)/shard_map/all_to_all | solution.py:43
  (76 shorter events, 11.5 us)
Async XLA Ops:
  8.0 9.8 %copy-start = (bf16[48,96]{1,0:T(8,128)(2,1)S(1)}, bf16[48,96]{1,0:T(8,128)(2,1)}, u32[]{:S(2)}) copy-start(bf16[48,96]{1,0:T(8,128)(2,1)} %param.6) | copy-start | bytes 27652
  8.0 107.0 %reduce-scatter.4.cloned.1.call-start = ((), (), s32[]{:S(2)}) async-start(), calls=%async_computation.8 | async-start | bytes 1769472 | tf_op jit(solution)/shard_map/reduce_scatter | solution.py:17
  12.6 1.4 copy-start.4
  12.6 201.1 %reduce-scatter.8.cloned.1.call-start = ((), (), s32[]{:S(2)}) async-start(), calls=%async_computation.12 | async-start | bytes 1769472 | tf_op jit(solution)/shard_map/reduce_scatter | solution.py:17
  15.3 0.7 copy-start.6
  15.3 26.4 %copy-start.5 = (bf16[1,6144,128]{2,1,0:T(8,128)(2,1)S(1)}, bf16[1,6144,128]{2,1,0:T(8,128)(2,1)}, u32[]{:S(2)}) copy-start(bf16[1,6144,128]{2,1,0:T(8,128)(2,1)} %param.10) | copy-start | bytes 4718596
  18.6 22.3 %all-to-all-start = ((bf16[8,8,96]{2,1,0:T(8,128)(2,1)}), bf16[8,8,96]{2,1,0:T(8,128)(2,1)S(1)}, u32[]{:S(2)}, u32[]{:S(2)}) async-start(bf16[8,8,96]{2,1,0:T(8,128)(2,1)} %fusion.28), calls=%async_computation | async-start | bytes 32768 | tf_op jit(solution)/shard_map/all_to_all | solution.py:115
  31.9 181.9 %all-gather.5.cloned.1.call-start = ((), (), s32[]{:S(2)}) async-start(), calls=%async_computation.7 | async-start | bytes 1597440 | tf_op jit(solution)/shard_map/all_gather | solution.py:25
  41.6 289.8 %reduce-scatter.6.cloned.1.call-start = ((), (), s32[]{:S(2)}) async-start(), calls=%async_computation.10 | async-start | bytes 1769472 | tf_op jit(solution)/shard_map/reduce_scatter | solution.py:17
  42.9 170.9 %copy-start.3 = (bf16[1,6144,128]{2,1,0:T(8,128)(2,1)S(1)}, bf16[1,6144,128]{2,1,0:T(8,128)(2,1)}, u32[]{:S(2)}) copy-start(bf16[1,6144,128]{2,1,0:T(8,128)(2,1)} %param.9) | copy-start | bytes 4718596
  43.0 307.5 %all-gather.7.cloned.1.call-start = ((), (), s32[]{:S(2)}) async-start(), calls=%async_computation.9 | async-start | bytes 1769472 | tf_op jit(solution)/shard_map/all_gather | solution.py:18
  115.0 237.9 %all-gather.11.cloned.1.call-start = ((), (), s32[]{:S(2)}) async-start(), calls=%async_computation.13 | async-start | bytes 1769472 | tf_op jit(solution)/shard_map/all_gather | solution.py:18
  213.8 2.1 copy-start.1
  219.9 111.7 %copy-start.7 = (s32[48,2]{0,1:T(2,128)S(1)}, s32[48,2]{0,1:T(2,128)}, u32[]{:S(2)}) copy-start(s32[48,2]{0,1:T(2,128)} %param.8) | copy-start | bytes 1156
  219.9 112.9 %all-to-all-start.1 = ((f32[8,8,6144]{2,1,0:T(8,128)}), f32[8,8,6144]{2,1,0:T(8,128)S(1)}, u32[]{:S(2)}, u32[]{:S(2)}) async-start(f32[8,8,6144]{2,1,0:T(8,128)} %fusion), calls=%async_computation.1 | async-start | bytes 3145728 | tf_op jit(solution)/shard_map/all_to_all | solution.py:127
  223.7 178.5 %all-gather.9.cloned.1.call-start = ((), (), s32[]{:S(2)}) async-start(), calls=%async_computation.11 | async-start | bytes 1769472 | tf_op jit(solution)/shard_map/all_gather | solution.py:18
  333.4 78.1 %all-to-all-start.3 = ((f32[8,2,8]{2,1,0:T(2,128)}), f32[8,2,8]{2,1,0:T(2,128)S(1)}, u32[]{:S(2)}, u32[]{:S(2)}) async-start(f32[8,2,8]{2,1,0:T(2,128)} %broadcast_in_dim.5), calls=%async_computation.6 | async-start | bytes 16384 | tf_op jit(solution)/shard_map/all_to_all | solution.py:49
  407.3 2.0 copy-start.2
  411.6 50.0 %all-to-all-start.2 = ((f32[64,48,96]{2,1,0:T(8,128)}), f32[64,48,96]{2,1,0:T(8,128)S(1)}, u32[]{:S(2)}, u32[]{:S(2)}) async-start(f32[64,48,96]{2,1,0:T(8,128)} %copy.65), calls=%async_computation.5 | async-start | bytes 3145728 | tf_op jit(solution)/shard_map/all_to_all | solution.py:43
Sparse Core Ops, SparseCore 0:
  13.4 101.5 reduce-scatter.3
  119.6 94.0 reduce-scatter.7
  218.4 113.0 reduce-scatter.5
Sparse Core Ops, SparseCore 1:
  41.7 119.9 all-gather.4
  164.7 75.4 all-gather.6
  243.3 80.9 all-gather.10
  331.5 70.5 all-gather.8
where the time goes:
time: 470 us
  waiting for transfers between devices  375 us (80%)
  starting transfers between devices  31.2 us (7%)
  local copies, waits for them, and re-layouts  20 us (4%)
  between operations  16.4 us (3%)
  other arithmetic  14.8 us (3%)
  matrix products  12.6 us (3%)
    reduce_scatter x3, waiting for transfers between devices, from_root(): own = lax.psum_scatter(padded, axis, scatter_dimension=0, tiled=True)  278 us
    all_gather x3, waiting for transfers between devices, from_root(): lax.all_gather(own, axis, axis=0, tiled=True)[:len(lines)]  49.3 us
    all_to_all x1, waiting for transfers between devices, sum_at_owner(): lax.all_to_all(split_up(value, dim, length), axis, 0, 0, tiled=True)  39.1 us
    all_to_all x1, starting transfers between devices, local(): lax.all_to_all(cold_send, 'expert', split_axis=0, concat_axis=0, tiled=True)  13.3 us
    dot_general x6, matrix products, matmul(): return jnp.dot(left, right, preferred_element_type=jnp.float32)  12.6 us
    all_to_all x1, starting transfers between devices, sum_at_owner(): lax.all_to_all(split_up(value, dim, length), axis, 0, 0, tiled=True)  10.4 us
  transfers between devices with their start and end apart: 11, of which 6 were waited for; matrix products, arithmetic and copies ran while one was open for 9% of the time, Pallas kernels for 0%

commit v1 on v0

--- a/solution.py
+++ b/solution.py
@@ -2,6 +2,11 @@
 import jax.numpy as jnp
 from jax import lax
 from jax.sharding import PartitionSpec as P
+
+
+def gather_over(value, axis, dim):
+    repeated = jnp.stack([value] * lax.axis_size(axis))
+    return jnp.concatenate(lax.all_to_all(repeated, axis, 0, 0), axis=dim)
 
 
 def filled_up(lines, length):
@@ -15,7 +20,7 @@
     )
     padded = filled_up(lines, lax.axis_size(axis))
     own = lax.psum_scatter(padded, axis, scatter_dimension=0, tiled=True)
-    return lax.all_gather(own, axis, axis=0, tiled=True)[: len(lines)].reshape(value.shape)
+    return gather_over(own, axis, 0)[: len(lines)].reshape(value.shape)
 
 
 def gather_turned(arrays, axis, dims):

time: 470 us -> 532 us (1.13)
  starting transfers between devices: 31.2 us -> 60.1 us
  waiting for transfers between devices: 375 us -> 398 us
    all_gather x1, waiting for transfers between devices: 0.02 us -> 114 us  [gather_turned(): out = lax.all_gather(both, axis, axis=0, tiled=True)]
    reduce_scatter x3, waiting for transfers between devices: 278 us -> 197 us  [from_root(): own = lax.psum_scatter(padded, axis, scatter_dimension=0, tiled=True)]
    all_gather x3 -> x0, waiting for transfers between devices: 49.3 us -> none  [from_root(): lax.all_gather(own, axis, axis=0, tiled=True)[:len(lines)]]
    all_to_all x1, waiting for transfers between devices: 0.01 us -> 28.4 us  [local(): lax.all_to_all(cold_part.reshape(experts, capacity, model_width), 'expert...]
    all_to_all x0 -> x3, starting transfers between devices: none -> 13 us  [gather_over(): return jnp.concatenate(lax.all_to_all(repeated, axis, 0, 0), axis=dim)]
    all_to_all x0 -> x3, waiting for transfers between devices: none -> 12.8 us  [gather_over(): return jnp.concatenate(lax.all_to_all(repeated, axis, 0, 0), axis=dim)]
    all_to_all x1, starting transfers between devices: 10.4 us -> 21.4 us  [sum_at_owner(): lax.all_to_all(split_up(value, dim, length), axis, 0, 0, tiled=True)]
    another operation x0 -> x3, local copies, waits for them, and re-layouts: none -> 6.8 us  [gather_over(): repeated = jnp.stack([value] * lax.axis_size(axis))]
  transfers between devices with their start and end apart: 11 -> 11, of which waited for: 6 -> 7; matrix products, arithmetic and copies ran while one was open for 9% -> 9% of each run, Pallas kernels for 0% -> 0%
where the time goes in v1:
time: 532 us; the launch traced here: 531 us
  waiting for transfers between devices  398 us (75%)
  starting transfers between devices  60.1 us (11%)
  local copies, waits for them, and re-layouts  25.3 us (5%)
  other arithmetic  18.1 us (3%)
  between operations  16.5 us (3%)
  matrix products  12.6 us (2%)
    reduce_scatter x3, waiting for transfers between devices, from_root(): own = lax.psum_scatter(padded, axis, scatter_dimension=0, tiled=True)  197 us
    all_gather x1, waiting for transfers between devices, gather_turned(): out = lax.all_gather(both, axis, axis=0, tiled=True)  114 us
    all_to_all x1, waiting for transfers between devices, sum_at_owner(): lax.all_to_all(split_up(value, dim, length), axis, 0, 0, tiled=True)  39.1 us
    all_to_all x1, waiting for transfers between devices, local(): lax.all_to_all(cold_part.reshape(experts, capacity, model_width), 'expert...  28.4 us
    all_to_all x1, starting transfers between devices, sum_at_owner(): lax.all_to_all(split_up(value, dim, length), axis, 0, 0, tiled=True)  21.4 us
    all_to_all x1, starting transfers between devices, local(): lax.all_to_all(cold_send, 'expert', split_axis=0, concat_axis=0, tiled=True)  13.3 us
    all_to_all x3, starting transfers between devices, gather_over(): return jnp.concatenate(lax.all_to_all(repeated, axis, 0, 0), axis=dim)  13 us
    all_to_all x3, waiting for transfers between devices, gather_over(): return jnp.concatenate(lax.all_to_all(repeated, axis, 0, 0), axis=dim)  12.8 us
  transfers between devices with their start and end apart: 11, of which 7 were waited for; matrix products, arithmetic and copies ran while one was open for 9% of the time, Pallas kernels for 0%

profile of v1, /device:TPU:1, one launch (start us, length us, event | category | flops | bytes accessed | tf_op | source)
XLA Modules:
  0.0 530.9 jit_solution(833503414291721951)
XLA Ops:
  12.5 13.3 %all-to-all-start = ((bf16[8,8,96]{2,1,0:T(8,128)(2,1)}), bf16[8,8,96]{2,1,0:T(8,128)(2,1)S(1)}, u32[]{:S(2)}, u32[]{:S(2)}) async-start(bf16[8,8,96]{2,1,0:T(8,128)(2,1)} %fusion.28), calls=%async_computation | async-start | bytes 32768 | tf_op jit(solution)/shard_map/all_to_all | solution.py:120
  27.6 7.2 %all-to-all-done = bf16[8,8,96]{2,1,0:T(8,128)(2,1)S(1)} async-done(((bf16[8,8,96]{2,1,0:T(8,128)(2,1)}), bf16[8,8,96]{2,1,0:T(8,128)(2,1)S(1)}, u32[]{:S(2)}, u32[]{:S(2)}) %all-to-all-start) | async-done | bytes 12320 | tf_op jit(solution)/shard_map/all_to_all | solution.py:120
  36.2 2.7 bitcast_select_fusion.2
  38.9 114.0 %all-gather.2.cloned.1.call-done = bf16[6144,106]{1,0:T(8,128)(2,1)} async-done(((bf16[96,106]{1,0:T(8,128)(2,1)}), bf16[6144,106]{1,0:T(8,128)(2,1)}) %all-gather.2.cloned.1.call-update) | async-done | bytes 1302544 | tf_op jit(solution)/shard_map/all_gather | solution.py:30
  155.1 3.9 fusion
  159.0 8.7 %all-to-all-start.1 = ((f32[8,8,6144]{2,1,0:T(8,128)}), f32[8,8,6144]{2,1,0:T(8,128)S(1)}, u32[]{:S(2)}, u32[]{:S(2)}) async-start(f32[8,8,6144]{2,1,0:T(8,128)} %fusion), calls=%async_computation.1 | async-start | bytes 3145728 | tf_op jit(solution)/shard_map/all_to_all | solution.py:132
  167.8 2.7 bitcast_select_fusion.1
  170.5 28.4 %all-to-all-done.1 = f32[8,8,6144]{2,1,0:T(8,128)S(1)} async-done(((f32[8,8,6144]{2,1,0:T(8,128)}), f32[8,8,6144]{2,1,0:T(8,128)S(1)}, u32[]{:S(2)}, u32[]{:S(2)}) %all-to-all-start.1) | async-done | bytes 1572896 | tf_op jit(solution)/shard_map/all_to_all | solution.py:132
  201.2 4.3 all-to-all-start.2
  205.6 2.7 bitcast_select_fusion
  208.2 97.3 %reduce-scatter.6.cloned.1.call-done = bf16[768,128]{1,0:T(8,128)(2,1)} async-done(((bf16[6144,128]{1,0:T(8,128)(2,1)}), bf16[768,128]{1,0:T(8,128)(2,1)}) %reduce-scatter.6.cloned.1.call-update) | async-done | bytes 196624 | tf_op jit(solution)/shard_map/reduce_scatter | solution.py:22
  305.6 2.3 stack.13
  307.9 4.3 all-to-all-start.3
  312.2 99.3 %reduce-scatter.8.cloned.1.call-done = bf16[16,6144]{1,0:T(8,128)(2,1)} async-done(((bf16[128,6144]{1,0:T(8,128)(2,1)}), bf16[16,6144]{1,0:T(8,128)(2,1)}) %reduce-scatter.8.cloned.1.call-update) | async-done | bytes 196624 | tf_op jit(solution)/shard_map/reduce_scatter | solution.py:22
  413.8 4.4 all-to-all-start.4
  419.6 2.7 gather_fusion
  422.3 3.7 gather.11
  425.9 5.0 multiply_reduce_fusion
  432.7 2.4 fusion.8
  435.2 12.8 %all-to-all-done.4 = bf16[8,16,6144]{2,1,0:T(8,128)(2,1)} async-done(((bf16[8,16,6144]{2,1,0:T(8,128)(2,1)}), bf16[8,16,6144]{2,1,0:T(8,128)(2,1)}, u32[]{:S(2)}, u32[]{:S(2)}) %all-to-all-start.4) | async-done | bytes 1572896 | tf_op jit(solution)/shard_map/all_to_all | solution.py:9
  448.6 3.5 all-to-all-start.6
  452.1 3.2 fusion.36
  461.6 21.4 %all-to-all-start.5 = ((f32[64,48,96]{2,1,0:T(8,128)}), f32[64,48,96]{2,1,0:T(8,128)S(1)}, u32[]{:S(2)}, u32[]{:S(2)}) async-start(f32[64,48,96]{2,1,0:T(8,128)} %copy.65), calls=%async_computation.8 | async-start | bytes 3145728 | tf_op jit(solution)/shard_map/all_to_all | solution.py:48
  483.6 39.1 %all-to-all-done.5 = f32[64,48,96]{2,1,0:T(8,128)S(1)} async-done(((f32[64,48,96]{2,1,0:T(8,128)}), f32[64,48,96]{2,1,0:T(8,128)S(1)}, u32[]{:S(2)}, u32[]{:S(2)}) %all-to-all-start.5) | async-done | bytes 1179680 | tf_op jit(solution)/shard_map/all_to_all | solution.py:48
  (72 shorter events, 25.1 us)
Async XLA Ops:
  8.0 3.8 copy-start
  12.5 22.3 %all-to-all-start = ((bf16[8,8,96]{2,1,0:T(8,128)(2,1)}), bf16[8,8,96]{2,1,0:T(8,128)(2,1)S(1)}, u32[]{:S(2)}, u32[]{:S(2)}) async-start(bf16[8,8,96]{2,1,0:T(8,128)(2,1)} %fusion.28), calls=%async_computation | async-start | bytes 32768 | tf_op jit(solution)/shard_map/all_to_all | solution.py:120
  25.8 127.1 %all-gather.2.cloned.1.call-start = ((), (), s32[]{:S(2)}) async-start(), calls=%async_computation.10 | async-start | bytes 1597440 | tf_op jit(solution)/shard_map/all_gather | solution.py:30
  35.5 135.0 %reduce-scatter.4.cloned.1.call-start = ((), (), s32[]{:S(2)}) async-start(), calls=%async_computation.11 | async-start | bytes 1769472 | tf_op jit(solution)/shard_map/reduce_scatter | solution.py:22
  38.9 114.0 %copy-start.3 = (bf16[1,6144,128]{2,1,0:T(8,128)(2,1)S(1)}, bf16[1,6144,128]{2,1,0:T(8,128)(2,1)}, u32[]{:S(2)}) copy-start(bf16[1,6144,128]{2,1,0:T(8,128)(2,1)} %param.9) | copy-start | bytes 4718596
  152.9 2.1 copy-start.1
  159.0 39.9 %all-to-all-start.1 = ((f32[8,8,6144]{2,1,0:T(8,128)}), f32[8,8,6144]{2,1,0:T(8,128)S(1)}, u32[]{:S(2)}, u32[]{:S(2)}) async-start(f32[8,8,6144]{2,1,0:T(8,128)} %fusion), calls=%async_computation.1 | async-start | bytes 3145728 | tf_op jit(solution)/shard_map/all_to_all | solution.py:132
  167.7 137.8 %reduce-scatter.6.cloned.1.call-start = ((), (), s32[]{:S(2)}) async-start(), calls=%async_computation.12 | async-start | bytes 1769472 | tf_op jit(solution)/shard_map/reduce_scatter | solution.py:22
  201.2 104.4 %all-to-all-start.2 = ((bf16[8,768,128]{2,1,0:T(8,128)(2,1)}), bf16[8,768,128]{2,1,0:T(8,128)(2,1)}, u32[]{:S(2)}, u32[]{:S(2)}) async-start(bf16[8,768,128]{2,1,0:T(8,128)(2,1)} %stack.12), calls=%async_computation.3 | async-start | bytes 3145728 | tf_op jit(solution)/shard_map/all_to_all | solution.py:9
  205.5 206.0 %reduce-scatter.8.cloned.1.call-start = ((), (), s32[]{:S(2)}) async-start(), calls=%async_computation.13 | async-start | bytes 1769472 | tf_op jit(solution)/shard_map/reduce_scatter | solution.py:22
  307.9 103.6 %all-to-all-start.3 = ((bf16[8,768,128]{2,1,0:T(8,128)(2,1)}), bf16[8,768,128]{2,1,0:T(8,128)(2,1)}, u32[]{:S(2)}, u32[]{:S(2)}) async-start(bf16[8,768,128]{2,1,0:T(8,128)(2,1)} %stack.13), calls=%async_computation.5 | async-start | bytes 3145728 | tf_op jit(solution)/shard_map/all_to_all | solution.py:9
  413.8 4.6 copy-start.5
  413.8 4.7 copy-start.4
  413.8 34.2 %all-to-all-start.4 = ((bf16[8,16,6144]{2,1,0:T(8,128)(2,1)}), bf16[8,16,6144]{2,1,0:T(8,128)(2,1)}, u32[]{:S(2)}, u32[]{:S(2)}) async-start(bf16[8,16,6144]{2,1,0:T(8,128)(2,1)} %stack.14), calls=%async_computation.7 | async-start | bytes 3145728 | tf_op jit(solution)/shard_map/all_to_all | solution.py:9
  448.6 13.0 %all-to-all-start.6 = ((f32[8,2,8]{2,1,0:T(2,128)}), f32[8,2,8]{2,1,0:T(2,128)S(1)}, u32[]{:S(2)}, u32[]{:S(2)}) async-start(f32[8,2,8]{2,1,0:T(2,128)} %broadcast_in_dim.5), calls=%async_computation.9 | async-start | bytes 16384 | tf_op jit(solution)/shard_map/all_to_all | solution.py:54
  457.2 2.0 copy-start.2
  461.6 61.0 %all-to-all-start.5 = ((f32[64,48,96]{2,1,0:T(8,128)}), f32[64,48,96]{2,1,0:T(8,128)S(1)}, u32[]{:S(2)}, u32[]{:S(2)}) async-start(f32[64,48,96]{2,1,0:T(8,128)} %copy.65), calls=%async_computation.8 | async-start | bytes 3145728 | tf_op jit(solution)/shard_map/all_to_all | solution.py:48
Sparse Core Ops, SparseCore 0:
  35.7 117.2 all-gather.1
Sparse Core Ops, SparseCore 1:
  40.6 94.1 reduce-scatter.3
  172.8 132.7 reduce-scatter.5
  310.1 101.4 reduce-scatter.7
